TPU v7x, 256 devices: a 4x2x16 block of a 4x16x16 slice. The times are simulated.
256 devices in a mesh: groups: 2 (over y), expert: 32 (over z, core), tensor: 4 (over x).
Axes of the slice: x: 4, y: 2, z: 16, core: 2. Of those that a mesh axis runs over, the one named last changes fastest.
The devices are a block of a 4x16x16 slice.
Arguments:
- tokens: bfloat16 [8192, 6144], P(('groups', 'expert', 'tensor')), parts along dimension 0, may hold values from -6 to 6
- expert_ids: int32 [8192, 2], P(('groups', 'expert', 'tensor')), parts along dimension 0, may hold values from 0 to 31, all different within a row; in each aligned block of 32 rows (0 to 31, 32 to 63, ...) at most 4 rows name the same one
- gate_scores: float32 [8192, 2], P(('groups', 'expert', 'tensor')), parts along dimension 0, may hold values from 0.1 to 1
- norm_gain: float32 [6144], replicated, may hold values from 0.1 to 1.9
- w_gate: bfloat16 [32, 6144, 1024], P('expert', None, 'tensor'), may hold values from -0.078125 to 0.078125
- w_up: bfloat16 [32, 6144, 1024], P('expert', None, 'tensor'), may hold values from -0.078125 to 0.078125
- w_down: bfloat16 [32, 1024, 6144], P('expert', 'tensor'), may hold values from -0.1875 to 0.1875
Outputs:
- mixed: bfloat16 [8192, 6144], P(('groups', 'expert', 'tensor')), parts along dimension 0
There are 2 independent parts, one for each index of `groups`. A program takes and returns all parts, laid end to end along the dimension named above; an argument that names none is the same for every part. Nothing has to cross between parts.
Inputs may be any that keep to these rules, and one draw needn't show every extreme that they name: `expert_ids`: each token names 2 different experts. Within the 32 tokens of one device, no expert is named more than 4 times, a bound that some block reaches.
All inputs are finite; a program needn't handle non-finite values.
Results may differ from a plain program's by a relative error of at most 0.011.
Values may be sent and summed in bfloat16 or wider, within the bound.
A program may use at most 64 MiB of HBM per device.

v0:
```python
import jax
import jax.numpy as jnp
from jax import lax
from jax.sharding import PartitionSpec as P


def on_device(tokens, expert_ids, gate_scores, norm_gain, w_gate, w_up, w_down):
    rows = tokens.shape[0]
    width = tokens.shape[1]
    picks = expert_ids.shape[1]
    experts = lax.axis_size("expert")
    capacity = 4 * rows // experts
    values = tokens.astype(jnp.float32)
    scale = lax.rsqrt(jnp.mean(values * values, axis=-1, keepdims=True) + 1e-05)
    normed = (values * scale * norm_gain).astype(jnp.bfloat16)
    flat_ids = expert_ids.reshape(-1)
    onehot = (flat_ids[:, None] == jnp.arange(experts, dtype=jnp.int32)[None, :]).astype(jnp.int32)
    earlier = jnp.cumsum(onehot, axis=0) - onehot
    slot = jnp.sum(earlier * onehot, axis=1)
    target = flat_ids * capacity + slot
    placing = jnp.arange(experts * capacity, dtype=jnp.int32)[:, None] == target[None, :]
    placing = placing.reshape(experts * capacity, rows, picks)
    place_tok = jnp.sum(placing.astype(jnp.float32), axis=2).astype(jnp.bfloat16)
    weighting = jnp.sum(placing.astype(jnp.float32) * gate_scores[None, :, :], axis=2)
    outgoing = jnp.dot(place_tok, normed, preferred_element_type=jnp.float32).astype(jnp.bfloat16)
    outgoing = outgoing.reshape(experts, capacity, width)
    arrived = lax.all_to_all(outgoing, "expert", split_axis=0, concat_axis=0, tiled=True)
    arrived = arrived.reshape(-1, width)
    piece = lax.all_gather(arrived, "tensor", axis=0, tiled=True)
    gate = jnp.dot(piece, w_gate[0], preferred_element_type=jnp.float32)
    up = jnp.dot(piece, w_up[0], preferred_element_type=jnp.float32)
    hidden = (jax.nn.silu(gate) * up).astype(jnp.bfloat16)
    parts = jnp.dot(hidden, w_down[0], preferred_element_type=jnp.float32)
    summed = lax.psum_scatter(parts.astype(jnp.bfloat16), "tensor", scatter_dimension=0, tiled=True)
    summed = summed.reshape(experts, capacity, width)
    results = lax.all_to_all(summed, "expert", split_axis=0, concat_axis=0, tiled=True)
    results = results.reshape(experts * capacity, width)
    mixed = jnp.dot(weighting.T, results.astype(jnp.float32), preferred_element_type=jnp.float32)
    return mixed.astype(jnp.bfloat16)


def solution(mesh):
    return jax.shard_map(
        on_device,
        mesh=mesh,
        in_specs=(
            P(("groups", "expert", "tensor"), None),
            P(("groups", "expert", "tensor"), None),
            P(("groups", "expert", "tensor"), None),
            P(),
            P("expert", None, "tensor"),
            P("expert", None, "tensor"),
            P("expert", "tensor", None),
        ),
        out_specs=P(("groups", "expert", "tensor"), None),
        check_vma=False,
    )
```

profile of v0, /device:TPU:33, one launch (start us, length us, event | category | flops | bytes accessed | tf_op | source)
XLA Modules:
  0.0 381.0 jit_solution(17998000077517687781)
XLA Ops:
  6.5 0.0 copy-start
  6.6 0.0 all-gather.2.cloned.1.call-start
  6.6 1.3 fusion.11
  7.9 0.8 copy.20
  8.7 0.1 eq.30
  8.8 0.1 fusion.17
  8.8 0.1 reduce_window_sum.11
  8.9 0.2 select_reduce_fusion.1
  9.1 0.1 reduce_sum.39
  9.2 0.1 copy.21
  9.3 0.7 multiply_add_fusion
  10.0 0.8 convert_reduce_fusion
  10.8 2.8 convolution_convert_fusion.1
  13.6 3.8 reshape.41
  17.4 103.9 %all_to_all.10 = bf16[32,4,6144]{2,1,0:T(4,128)(2,1)} all-to-all(bf16[32,4,6144]{2,1,0:T(4,128)(2,1)} %reshape.41), channel_id=1, replica_groups=mesh['groups'=2,'expert'=32,'tensor'=4] {'expert'}, dimensions={0} | all-to-all | bytes 3145728 | tf_op jit(solution)/shard_map/all_to_all | solution.py:27
  121.2 3.6 reshape.42
  124.9 0.1 all-gather.2.cloned.1.call-update
  124.9 0.1 reduce-scatter.2.cloned.1.call-start
  125.0 63.8 %all-gather.2.cloned.1.call-done = bf16[512,6144]{1,0:T(8,128)(2,1)} async-done(((bf16[128,6144]{1,0:T(8,128)(2,1)}), bf16[512,6144]{1,0:T(8,128)(2,1)}) %all-gather.2.cloned.1.call-update) | async-done | bytes 6291472 | tf_op jit(solution)/shard_map/all_gather | solution.py:29
  188.8 0.0 copy-start.1
  188.8 0.0 copy-start.2
  188.8 5.6 %fusion.3 = f32[512,256]{1,0:T(8,128)S(1)} fusion(bf16[512,6144]{1,0:T(8,128)(2,1)} %all-gather.2.cloned.1.call-done, bf16[1,6144,256]{2,1,0:T(8,128)(2,1)} %param.11), kind=kOutput, calls=%fused_computation.6 | convolution fusion | flops 1610612736 | bytes 9961472 | tf_op jit(solution)/shard_map/dot_general | solution.py:30
  194.5 0.0 copy-done.1
  194.5 0.8 copy-done.2
  195.3 1.8 fusion.8
  197.0 0.0 copy-done
  197.1 4.5 %convolution_convert_fusion = bf16[512,6144]{1,0:T(8,128)(2,1)} fusion(bf16[512,256]{1,0:T(8,128)(2,1)S(1)} %fusion.8, bf16[1,256,6144]{2,1,0:T(8,128)(2,1)S(1)} %copy-done), kind=kOutput, calls=%fused_computation | convolution fusion | flops 1613758464 | bytes 9699328 | tf_op jit(solution)/shard_map/dot_general | solution.py:33
  201.5 0.1 reduce-scatter.2.cloned.1.call-update
  201.6 71.0 %reduce-scatter.2.cloned.1.call-done = bf16[128,6144]{1,0:T(8,128)(2,1)} async-done(((bf16[512,6144]{1,0:T(8,128)(2,1)}), bf16[128,6144]{1,0:T(8,128)(2,1)}) %reduce-scatter.2.cloned.1.call-update) | async-done | bytes 1572880 | tf_op jit(solution)/shard_map/reduce_scatter | solution.py:34
  272.6 3.8 reshape.43
  276.4 91.6 %all_to_all.11 = bf16[32,4,6144]{2,1,0:T(4,128)(2,1)} all-to-all(bf16[32,4,6144]{2,1,0:T(4,128)(2,1)} %reshape.43), channel_id=1, replica_groups=mesh['groups'=2,'expert'=32,'tensor'=4] {'expert'}, dimensions={0} | all-to-all | bytes 3145728 | tf_op jit(solution)/shard_map/all_to_all | solution.py:36
  368.0 3.7 reshape.44
  371.6 2.5 fusion.19
  (1 shorter events, 0.0 us)
Async XLA Ops:
  6.5 190.5 %copy-start = (bf16[1,256,6144]{2,1,0:T(8,128)(2,1)S(1)}, bf16[1,256,6144]{2,1,0:T(8,128)(2,1)}, u32[]{:S(2)}) copy-start(bf16[1,256,6144]{2,1,0:T(8,128)(2,1)} %param.13) | copy-start | bytes 9437188
  6.6 182.3 %all-gather.2.cloned.1.call-start = ((), (), s32[]{:S(2)}) async-start(), calls=%async_computation.3 | async-start | bytes 7864320 | tf_op jit(solution)/shard_map/all_gather | solution.py:29
  124.9 147.7 %reduce-scatter.2.cloned.1.call-start = ((), (), s32[]{:S(2)}) async-start(), calls=%async_computation.4 | async-start | bytes 7864320 | tf_op jit(solution)/shard_map/reduce_scatter | solution.py:34
  188.8 5.7 %copy-start.1 = (bf16[512,6144]{1,0:T(8,128)(2,1)S(1)}, bf16[512,6144]{1,0:T(8,128)(2,1)}, u32[]{:S(2)}) copy-start(bf16[512,6144]{1,0:T(8,128)(2,1)} %all-gather.2.cloned.1.call-done) | copy-start | bytes 18874372
  188.8 6.4 %copy-start.2 = (bf16[1,6144,256]{2,1,0:T(8,128)(2,1)S(1)}, bf16[1,6144,256]{2,1,0:T(8,128)(2,1)}, u32[]{:S(2)}) copy-start(bf16[1,6144,256]{2,1,0:T(8,128)(2,1)} %param.12) | copy-start | bytes 9437188
Sparse Core Ops, SparseCore 0:
  125.0 63.7 all-gather.1
  201.7 70.8 reduce-scatter.1
where the time goes:
time: 382 us; the launch traced here: 381 us
  blocking collectives  195 us (51%)
  waiting for transfers between devices  135 us (35%)
  matrix products  17.2 us (5%)
  local copies, waits for them, and re-layouts  16.7 us (4%)
  between operations  13.5 us (4%)
    all_to_all x1, blocking collectives, on_device(): lax.all_to_all(outgoing, 'expert', split_axis=0, concat_axis=0, tiled=True)  104 us
    all_to_all x1, blocking collectives, on_device(): lax.all_to_all(summed, 'expert', split_axis=0, concat_axis=0, tiled=True)  91.6 us
    reduce_scatter x1, waiting for transfers between devices, on_device(): lax.psum_scatter(parts.astype(jnp.bfloat16), 'tensor', scatter_dimension=...  71 us
    all_gather x1, waiting for transfers between devices, on_device(): piece = lax.all_gather(arrived, 'tensor', axis=0, tiled=True)  63.8 us
  transfers between devices with their start and end apart: 2, of which 2 were waited for; matrix products, arithmetic and copies ran while one was open for 0% of the time, Pallas kernels for 0%

commit v1 on v0

--- a/solution.py
+++ b/solution.py
@@ -26,7 +26,8 @@
     outgoing = outgoing.reshape(experts, capacity, width)
     arrived = lax.all_to_all(outgoing, "expert", split_axis=0, concat_axis=0, tiled=True)
     arrived = arrived.reshape(-1, width)
-    piece = lax.all_gather(arrived, "tensor", axis=0, tiled=True)
+    copies = jnp.concatenate([arrived] * lax.axis_size("tensor"), axis=0)
+    piece = lax.all_to_all(copies, "tensor", 0, 0, tiled=True)
     gate = jnp.dot(piece, w_gate[0], preferred_element_type=jnp.float32)
     up = jnp.dot(piece, w_up[0], preferred_element_type=jnp.float32)
     hidden = (jax.nn.silu(gate) * up).astype(jnp.bfloat16)

time: 382 us -> 382 us (level)
  blocking collectives: 195 us -> 270 us
  waiting for transfers between devices: 135 us -> 61.4 us
  other arithmetic: 3.14 us -> 7.12 us
  matrix products: 17.2 us -> 13.3 us
    all_to_all x0 -> x1, blocking collectives: none -> 74.6 us  [on_device(): piece = lax.all_to_all(copies, 'tensor', 0, 0, tiled=True)]
    all_gather x1 -> x0, waiting for transfers between devices: 63.8 us -> none  [on_device(): piece = lax.all_gather(arrived, 'tensor', axis=0, tiled=True)]
    reduce_scatter x1, waiting for transfers between devices: 71 us -> 61.3 us  [on_device(): lax.psum_scatter(parts.astype(jnp.bfloat16), 'tensor', scatter_dimension=...]
    concatenate x0 -> x1, other arithmetic: none -> 3.98 us  [on_device(): copies = jnp.concatenate([arrived] * lax.axis_size('tensor'), axis=0)]
    dot_general x1, matrix products: 5.64 us -> 1.79 us  [on_device(): gate = jnp.dot(piece, w_gate[0], preferred_element_type=jnp.float32)]
  transfers between devices with their start and end apart: 2 -> 1, of which waited for: 2 -> 1; matrix products, arithmetic and copies ran while one was open for 0% -> 0% of each run, Pallas kernels for 0% -> 0%
where the time goes in v1:
time: 382 us; the launch traced here: 381 us
  blocking collectives  270 us (71%)
  waiting for transfers between devices  61.4 us (16%)
  local copies, waits for them, and re-layouts  16.1 us (4%)
  between operations  13.5 us (4%)
  matrix products  13.3 us (3%)
  other arithmetic  7.12 us (2%)
    all_to_all x1, blocking collectives, on_device(): lax.all_to_all(outgoing, 'expert', split_axis=0, concat_axis=0, tiled=True)  104 us
    all_to_all x1, blocking collectives, on_device(): lax.all_to_all(summed, 'expert', split_axis=0, concat_axis=0, tiled=True)  91.6 us
    all_to_all x1, blocking collectives, on_device(): piece = lax.all_to_all(copies, 'tensor', 0, 0, tiled=True)  74.6 us
    reduce_scatter x1, waiting for transfers between devices, on_device(): lax.psum_scatter(parts.astype(jnp.bfloat16), 'tensor', scatter_dimension=...  61.3 us
  transfers between devices with their start and end apart: 1, of which 1 were waited for; matrix products, arithmetic and copies ran while one was open for 0% of the time, Pallas kernels for 0%

profile of v1, /device:TPU:33, one launch (start us, length us, event | category | flops | bytes accessed | tf_op | source)
XLA Modules:
  0.0 381.5 jit_solution(9887857108300863155)
XLA Ops:
  6.5 0.0 copy-start
  6.6 0.0 reduce-scatter.2.cloned.1.call-start
  6.6 1.3 fusion.11
  7.9 0.8 copy.20
  8.7 0.1 eq.30
  8.8 0.1 fusion.17
  8.8 0.1 reduce_window_sum.11
  8.9 0.2 select_reduce_fusion.1
  9.1 0.1 reduce_sum.39
  9.2 0.1 copy.21
  9.3 0.7 multiply_add_fusion
  10.0 0.8 convert_reduce_fusion
  10.8 2.8 convolution_convert_fusion.1
  13.6 3.8 reshape.43
  17.4 103.9 %all_to_all.22 = bf16[32,4,6144]{2,1,0:T(4,128)(2,1)} all-to-all(bf16[32,4,6144]{2,1,0:T(4,128)(2,1)} %reshape.43), channel_id=1, replica_groups=mesh['groups'=2,'expert'=32,'tensor'=4] {'expert'}, dimensions={0} | all-to-all | bytes 3145728 | tf_op jit(solution)/shard_map/all_to_all | solution.py:27
  121.2 3.7 reshape.44
  124.9 4.0 %pad_maximum_fusion = bf16[512,6144]{1,0:T(8,128)(2,1)S(1)} fusion(bf16[128,6144]{1,0:T(8,128)(2,1)} %reshape.44), kind=kLoop, calls=%fused_computation.3 | loop fusion | flops 25165824 | bytes 7864320 | tf_op jit(solution)/shard_map/concatenate | solution.py:29
  128.9 0.0 copy-start.1
  128.9 74.6 %all_to_all.23 = bf16[4,128,6144]{2,1,0:T(8,128)(2,1)S(1)} all-to-all(bf16[4,128,6144]{2,1,0:T(8,128)(2,1)S(1)} %bitcast.21), channel_id=1, replica_groups=mesh['groups'=2,'expert'=32,'tensor'=4] {'tensor'}, dimensions={0} | all-to-all | bytes 12582912 | tf_op jit(solution)/shard_map/all_to_all | solution.py:30
  203.5 0.0 copy-done.1
  203.5 0.0 copy-start.2
  203.5 1.8 fusion.3
  205.3 0.1 copy-done.2
  205.4 1.8 fusion.8
  207.2 0.0 copy-done
  207.2 4.5 %convolution_convert_fusion = bf16[512,6144]{1,0:T(8,128)(2,1)} fusion(bf16[512,256]{1,0:T(8,128)(2,1)S(1)} %fusion.8, bf16[1,256,6144]{2,1,0:T(8,128)(2,1)S(1)} %copy-done), kind=kOutput, calls=%fused_computation | convolution fusion | flops 1613758464 | bytes 9699328 | tf_op jit(solution)/shard_map/dot_general | solution.py:34
  211.7 0.1 reduce-scatter.2.cloned.1.call-update
  211.8 61.3 %reduce-scatter.2.cloned.1.call-done = bf16[128,6144]{1,0:T(8,128)(2,1)} async-done(((bf16[512,6144]{1,0:T(8,128)(2,1)}), bf16[128,6144]{1,0:T(8,128)(2,1)}) %reduce-scatter.2.cloned.1.call-update) | async-done | bytes 1572880 | tf_op jit(solution)/shard_map/reduce_scatter | solution.py:35
  273.1 3.8 reshape.45
  276.9 91.6 %all_to_all.24 = bf16[32,4,6144]{2,1,0:T(4,128)(2,1)} all-to-all(bf16[32,4,6144]{2,1,0:T(4,128)(2,1)} %reshape.45), channel_id=1, replica_groups=mesh['groups'=2,'expert'=32,'tensor'=4] {'expert'}, dimensions={0} | all-to-all | bytes 3145728 | tf_op jit(solution)/shard_map/all_to_all | solution.py:37
  368.5 3.7 reshape.46
  372.1 2.5 fusion.19
  (1 shorter events, 0.0 us)
Async XLA Ops:
  6.5 200.7 %copy-start = (bf16[1,256,6144]{2,1,0:T(8,128)(2,1)S(1)}, bf16[1,256,6144]{2,1,0:T(8,128)(2,1)}, u32[]{:S(2)}) copy-start(bf16[1,256,6144]{2,1,0:T(8,128)(2,1)} %param.13) | copy-start | bytes 9437188
  6.6 266.5 %reduce-scatter.2.cloned.1.call-start = ((), (), s32[]{:S(2)}) async-start(), calls=%async_computation.4 | async-start | bytes 7864320 | tf_op jit(solution)/shard_map/reduce_scatter | solution.py:35
  128.9 74.7 %copy-start.1 = (bf16[1,6144,256]{2,1,0:T(8,128)(2,1)S(1)}, bf16[1,6144,256]{2,1,0:T(8,128)(2,1)}, u32[]{:S(2)}) copy-start(bf16[1,6144,256]{2,1,0:T(8,128)(2,1)} %param.11) | copy-start | bytes 9437188
  203.5 1.9 copy-start.2
Sparse Core Ops, SparseCore 0:
  211.9 61.1 reduce-scatter.1
